TPU v7x, 32 devices: a whole 2x2x4 slice. The times are simulated.
32 devices in a mesh: blk: 4 (over y, x), grp: 8 (over z, core).
Axes of the slice: x: 2, y: 2, z: 4, core: 2. Of those that a mesh axis runs over, the one named last changes fastest.
Arguments:
- points: float32 [3, 4096], P(None, ('blk', 'grp')), may hold values from 0 to 1
- labels: int32 [4096], P(('blk', 'grp')), may hold values 0 or 1
- shape_scale: float32 [4096], P(('blk', 'grp')), may hold values from 0.1 to 0.4
- krylov_basis: float32 [8, 32, 4096], P(None, None, ('blk', 'grp')), may hold values from -6 to 6
- sketch: float32 [1024, 4096], P(None, ('blk', 'grp')), may hold values from -0.09375 to 0.09375
- sketched_basis: float32 [8, 32, 1024], replicated, may hold values from -0.1875 to 0.1875
Outputs:
- next_vector: float32 [32, 4096], P(None, ('blk', 'grp'))
- coefficients: float32 [8, 32], replicated
- sketch_next: float32 [32, 1024], replicated
- norms: float32 [32], replicated
All inputs are finite; a program needn't handle non-finite values. No bound on the sum of `labels` on one device may be relied on, other than what follows from the above.
Results may differ from a plain program's by a relative error of at most 0.0003.
Values sent between devices are 32-bit elements; how exact they have to be, the bound alone decides.
A program may use at most 64 MiB of HBM per device.

v0:
```python
import math
import jax
import jax.numpy as jnp
from jax import lax
from jax.sharding import PartitionSpec as P

SYSTEMS = 32
KRYLOV = 8


def kernel_terms(target_points, target_labels, source_block):
    source_points = source_block[0:3]
    scales = source_block[3]
    weights_block = source_block[4:]
    delta_x = source_points[0][:, None] - target_points[0][None, :]
    delta_y = source_points[1][:, None] - target_points[1][None, :]
    delta_z = source_points[2][:, None] - target_points[2][None, :]
    radius_sq = delta_x * delta_x + delta_y * delta_y + delta_z * delta_z
    squared_scale = (scales * scales)[:, None]
    shifted = radius_sq + squared_scale
    inverse = lax.rsqrt(shifted)
    boundary = shifted * inverse
    interior = (3.0 * squared_scale + 2.0 * radius_sq) * inverse * inverse * inverse
    kernel = jnp.where(target_labels[None, :] == 1, interior, boundary)
    return jnp.dot(
        weights_block, kernel, precision=lax.Precision.HIGHEST, preferred_element_type=jnp.float32
    )


def block_size(length, wanted):
    return wanted if length % wanted == 0 else length


def accumulate(running, target_points, target_labels, source_block):
    target_count = target_points.shape[1]
    source_count = source_block.shape[1]
    tblock = block_size(target_count, 2048)
    sblock = block_size(source_count, 2048)
    system_rows = running.shape[0]

    def over_targets(target_index, current):

        def over_sources(source_index, partial_value):
            portion = lax.dynamic_slice_in_dim(source_block, source_index * sblock, sblock, 1)
            return partial_value + kernel_terms(target_points, target_labels, portion)

        partial_value = lax.fori_loop(
            0, source_count // sblock, over_sources, jnp.zeros((system_rows, tblock), jnp.float32)
        )
        return current + partial_value

    return lax.fori_loop(0, target_count // tblock, over_targets, running)


def shards(points, labels, shape_scale, krylov_basis, sketch, sketched_basis):
    own_count = points.shape[1]
    everything = lax.axis_size("blk") * lax.axis_size("grp") * own_count
    sources = jnp.concatenate([points, shape_scale[None, :], krylov_basis[KRYLOV - 1]], axis=0)
    empty = jnp.zeros((SYSTEMS, own_count), jnp.float32)
    summed = accumulate(
        empty, points, labels, lax.all_gather(sources, ("blk", "grp"), axis=1, tiled=True)
    )
    image = summed / math.sqrt(everything)
    local_sketch = lax.dot_general(
        image,
        sketch,
        (((1,), (1,)), ((), ())),
        precision=lax.Precision.HIGHEST,
        preferred_element_type=jnp.float32,
    )
    sketched = lax.psum(local_sketch, ("blk", "grp"))
    coefficients = jnp.einsum(
        "jrk,rk->jr", sketched_basis, sketched, precision=lax.Precision.HIGHEST
    )
    remainder = sketched - jnp.einsum(
        "jr,jrk->rk", coefficients, sketched_basis, precision=lax.Precision.HIGHEST
    )
    norms = jnp.sqrt(jnp.mean(remainder * remainder, axis=1) + 1e-06)
    sketch_next = remainder / norms[:, None]
    reduced = image - jnp.einsum(
        "jr,jrn->rn", coefficients, krylov_basis, precision=lax.Precision.HIGHEST
    )
    next_vector = reduced / norms[:, None]
    return (next_vector, coefficients, sketch_next, norms)


def solution(mesh):
    placed = (
        P(None, ("blk", "grp")),
        P(("blk", "grp")),
        P(("blk", "grp")),
        P(None, None, ("blk", "grp")),
        P(None, ("blk", "grp")),
        P(),
    )
    return jax.shard_map(
        shards,
        mesh=mesh,
        in_specs=placed,
        out_specs=(P(None, ("blk", "grp")), P(), P(), P()),
        check_vma=False,
    )
```

profile of v0, /device:TPU:0, one launch (start us, length us, event | category | flops | bytes accessed | tf_op | source)
XLA Modules:
  0.0 195.9 jit_solution(17373773227067051160)
XLA Ops:
  7.2 0.0 copy-start
  7.2 0.0 all-reduce.2.cloned.1.call-start
  7.2 0.0 copy-start.4
  7.2 0.8 slice_bitcast_fusion.3
  8.1 0.0 copy-done.4
  8.1 0.7 copy-done.7
  8.7 45.9 %all_gather.3 = f32[36,4096]{1,0:T(8,128)S(1)} all-gather(f32[36,128]{1,0:T(8,128)S(1)} %pad_maximum_fusion), channel_id=1, replica_groups=mesh['blk'=4,'grp'=8] {'blk','grp'}, dimensions={1}, use_global_device_ids=true | all-gather | bytes 608256 | tf_op jit(solution)/shard_map/all_gather | solution.py:61
  54.7 4.4 %while.21 = (s32[]{:T(128)}, f32[32,128]{1,0:T(8,128)S(1)}, f32[36,4096]{1,0:T(8,128)S(1)}, s32[128]{0:T(128)S(1)}, f32[3,128]{1,0:T(4,128)S(1)}, /*index=5*/s32...) while((s32[]{:T(128)}, f32[32,128]{1,0:T(8,128)S(1)}, ...), condition=%wide.region_1.0_spmd.clone, body=%wide.region_0.1_spmd.clone.sunk | while | flops 104870024 | bytes 423813 | solution.py:47
  54.7 0.1 constant_dynamic-slice_fusion.2
  54.8 2.0 %convolution_add_fusion.2 = f32[32,128]{1,0:T(8,128)S(1)} fusion(f32[2048]{0:T(1024)S(1)} %bitcast.42, f32[128]{0:T(128)S(1)} %get-tuple-element.195, f32[2048]{0:T(1024)S(1)} %bitcast.45, f32[128]{0:T(128)S(1)} %get-tuple-element.197, f32[2048]{0:T(1024)S(1)} %bitcast.44, f32[128]{0:T(128)S(1)} %get-tuple-element.199, f32[2048]{0:T(1024)S(1)} %bitcast.43, ...), kind=kOutput, calls=%fused_computation.2.clone.1 | convolution fusion | flops 104865792 | bytes 337929 | tf_op jit(solution)/shard_map/while/body/eval_jaxpr/while/body/eval_jaxpr/dot_general | solution.py:25
  56.9 0.1 constant_dynamic-slice_fusion.2
  57.0 2.0 %convolution_add_fusion.2 = f32[32,128]{1,0:T(8,128)S(1)} fusion(f32[2048]{0:T(1024)S(1)} %bitcast.42, f32[128]{0:T(128)S(1)} %get-tuple-element.195, f32[2048]{0:T(1024)S(1)} %bitcast.45, f32[128]{0:T(128)S(1)} %get-tuple-element.197, f32[2048]{0:T(1024)S(1)} %bitcast.44, f32[128]{0:T(128)S(1)} %get-tuple-element.199, f32[2048]{0:T(1024)S(1)} %bitcast.43, ...), kind=kOutput, calls=%fused_computation.2.clone.1 | convolution fusion | flops 104865792 | bytes 337929 | tf_op jit(solution)/shard_map/while/body/eval_jaxpr/while/body/eval_jaxpr/dot_general | solution.py:25
  59.1 1.3 fusion.32
  60.3 0.0 all-reduce.2.cloned.1.call-update
  60.4 120.9 %all-reduce.2.cloned.1.call-done = f32[32,1024]{1,0:T(8,128)} async-done(((f32[32,1024]{1,0:T(8,128)}), f32[32,1024]{1,0:T(8,128)}) %all-reduce.2.cloned.1.call-update) | async-done | bytes 131088 | tf_op jit(solution)/shard_map/psum | solution.py:71
  181.3 3.6 %fusion.27 = f32[32,1,8]{2,1,0:T(1,128)S(1)} fusion(f32[8,32,1024]{2,1,0:T(8,128)S(1)} %copy-done, f32[32,1024,1]{1,0,2:T(8,128)} %bitcast.40), kind=kOutput, calls=%fused_computation.36 | convolution fusion | flops 3145728 | bytes 1180672 | tf_op jit(solution)/shard_map/jrk,rk->jr/dot_general | solution.py:72
  184.8 0.1 copy.12
  184.9 0.1 copy.13
  185.0 0.5 copy-done.5
  185.5 0.4 fusion.29
  185.9 1.5 fusion.25
  187.4 0.1 multiply_reduce_fusion
  187.6 0.7 subtract_divide_fusion
  188.3 0.7 broadcast_divide_fusion
  (22 shorter events, 0.1 us)
Async XLA Ops:
  7.2 174.1 %copy-start = (f32[8,32,1024]{2,1,0:T(8,128)S(1)}, f32[8,32,1024]{2,1,0:T(8,128)}, u32[]{:S(2)}) copy-start(f32[8,32,1024]{2,1,0:T(8,128)} %param.13) | copy-start | bytes 3145732
  7.2 174.1 %all-reduce.2.cloned.1.call-start = ((), (), s32[]{:S(2)}) async-start(), calls=%async_computation | async-start | bytes 262144 | tf_op jit(solution)/shard_map/psum | solution.py:71
  7.2 0.8 copy-start.4
  8.0 0.7 copy-start.7
  8.7 46.0 %copy-start.8 = (s32[128]{0:T(128)S(1)}, s32[128]{0:T(128)}, u32[]{:S(2)}) copy-start(s32[128]{0:T(128)} %param.9) | copy-start | bytes 1540
  54.7 4.4 %copy-start.2 = (f32[1024,128]{1,0:T(8,128)S(1)}, f32[1024,128]{1,0:T(8,128)}, u32[]{:S(2)}) copy-start(f32[1024,128]{1,0:T(8,128)} %param.12) | copy-start | bytes 1572868
  181.2 4.3 %copy-start.3 = (f32[8,32,128]{2,1,0:T(8,128)S(1)}, f32[8,32,128]{2,1,0:T(8,128)}, u32[]{:S(2)}) copy-start(f32[8,32,128]{2,1,0:T(8,128)} %param.11) | copy-start | bytes 393220
  184.9 0.6 copy-start.5
  185.9 1.5 copy-start.1
  187.6 0.7 copy-start.6
Sparse Core Ops, SparseCore 0:
  60.5 120.7 all-reduce.1
where the time goes:
time: 196 us
  waiting for transfers between devices  121 us (62%)
  blocking collectives  45.9 us (23%)
  between operations  14.1 us (7%)
  matrix products  10.7 us (5%)
  local copies, waits for them, and re-layouts  2.17 us (1%)
    psum x1, waiting for transfers between devices, shards(): sketched = lax.psum(local_sketch, ('blk', 'grp'))  121 us
    all_gather x1, blocking collectives, shards(): lax.all_gather(sources, ('blk', 'grp'), axis=1, tiled=True)  45.9 us
    dot_general x2, matrix products, kernel_terms(): jnp.dot(weights_block, kernel, precision=lax.Precision.HIGHEST, preferred...  4 us
  transfers between devices with their start and end apart: 1, of which 1 were waited for; matrix products, arithmetic and copies ran while one was open for 0% of the time, Pallas kernels for 0%

commit v1 on v0

--- a/solution.py
+++ b/solution.py
@@ -6,6 +6,12 @@
 
 SYSTEMS = 32
 KRYLOV = 8
+
+
+def play_tokens(slab_in):
+    u1 = lax.all_gather(slab_in, ("blk", "grp"))
+    passed = jnp.sum(u1, axis=0)
+    return passed
 
 
 def kernel_terms(target_points, target_labels, source_block):
@@ -68,7 +74,7 @@
         precision=lax.Precision.HIGHEST,
         preferred_element_type=jnp.float32,
     )
-    sketched = lax.psum(local_sketch, ("blk", "grp"))
+    sketched = play_tokens(local_sketch)
     coefficients = jnp.einsum(
         "jrk,rk->jr", sketched_basis, sketched, precision=lax.Precision.HIGHEST
     )

time: 196 us -> 137 us (0.70)
  waiting for transfers between devices: 121 us -> 58.1 us
  other arithmetic: 1.87 us -> 6.34 us
    psum x1 -> x0, waiting for transfers between devices: 121 us -> none  [shards(): sketched = lax.psum(local_sketch, ('blk', 'grp'))]
    all_gather x0 -> x1, waiting for transfers between devices: none -> 58.1 us  [play_tokens(): u1 = lax.all_gather(slab_in, ('blk', 'grp'))]
    reduce_sum x0 -> x1, other arithmetic: none -> 2.43 us  [play_tokens(): passed = jnp.sum(u1, axis=0)]
where the time goes in v1:
time: 137 us
  waiting for transfers between devices  58.1 us (42%)
  blocking collectives  45.9 us (34%)
  between operations  14.1 us (10%)
  matrix products  9.92 us (7%)
  other arithmetic  6.34 us (5%)
  local copies, waits for them, and re-layouts  2.56 us (2%)
    all_gather x1, waiting for transfers between devices, play_tokens(): u1 = lax.all_gather(slab_in, ('blk', 'grp'))  58.1 us
    all_gather x1, blocking collectives, shards(): lax.all_gather(sources, ('blk', 'grp'), axis=1, tiled=True)  45.9 us
    dot_general x2, matrix products, kernel_terms(): jnp.dot(weights_block, kernel, precision=lax.Precision.HIGHEST, preferred...  4 us
    dot_general x1, matrix products, shards(): jnp.einsum('jrk,rk->jr', sketched_basis, sketched, precision=lax.Precisio...  2.74 us
  transfers between devices with their start and end apart: 1, of which 1 were waited for; matrix products, arithmetic and copies ran while one was open for 0% of the time, Pallas kernels for 0%

profile of v1, /device:TPU:0, one launch (start us, length us, event | category | flops | bytes accessed | tf_op | source)
XLA Modules:
  0.0 137.0 jit_solution(6235236021583655064)
XLA Ops:
  7.2 0.0 all-gather.3.cloned.1.call-start
  7.2 0.8 slice_bitcast_fusion.3
  8.0 0.7 pad_maximum_fusion
  8.7 45.9 %all_gather.9 = f32[36,4096]{1,0:T(8,128)S(1)} all-gather(f32[36,128]{1,0:T(8,128)S(1)} %pad_maximum_fusion), channel_id=1, replica_groups=mesh['blk'=4,'grp'=8] {'blk','grp'}, dimensions={1}, use_global_device_ids=true | all-gather | bytes 608256 | tf_op jit(solution)/shard_map/all_gather | solution.py:67
  54.7 7.3 %while.21 = (s32[]{:T(128)}, f32[32,128]{1,0:T(8,128)S(1)}, f32[36,4096]{1,0:T(8,128)S(1)}, s32[128]{0:T(128)}, f32[3,128]{1,0:T(4,128)}, /*index=5*/s32[]{:T(12...) while((s32[]{:T(128)}, f32[32,128]{1,0:T(8,128)S(1)}, ...), condition=%wide.region_1.0_spmd.clone, body=%wide.region_0.1_spmd.clone.sunk | while | flops 104870024 | bytes 423813 | solution.py:53
  54.7 0.7 broadcast_compare_fusion.2
  55.4 0.8 slice_bitcast_fusion.5
  56.2 0.1 constant_dynamic-slice_fusion.2
  56.3 2.0 %convolution_add_fusion.2 = f32[32,128]{1,0:T(8,128)S(1)} fusion(f32[2048]{0:T(1024)S(1)} %bitcast.44, f32[128]{0:T(128)S(1)} %get-tuple-element.195, f32[2048]{0:T(1024)S(1)} %bitcast.47, f32[128]{0:T(128)S(1)} %get-tuple-element.197, f32[2048]{0:T(1024)S(1)} %bitcast.46, f32[128]{0:T(128)S(1)} %get-tuple-element.199, f32[2048]{0:T(1024)S(1)} %bitcast.45, ...), kind=kOutput, calls=%fused_computation.2.clone.1 | convolution fusion | flops 104865792 | bytes 337929 | tf_op jit(solution)/shard_map/while/body/eval_jaxpr/while/body/eval_jaxpr/dot_general | solution.py:31
  58.3 0.7 broadcast_compare_fusion.2
  59.0 0.8 slice_bitcast_fusion.5
  59.8 0.1 constant_dynamic-slice_fusion.2
  59.9 2.0 %convolution_add_fusion.2 = f32[32,128]{1,0:T(8,128)S(1)} fusion(f32[2048]{0:T(1024)S(1)} %bitcast.44, f32[128]{0:T(128)S(1)} %get-tuple-element.195, f32[2048]{0:T(1024)S(1)} %bitcast.47, f32[128]{0:T(128)S(1)} %get-tuple-element.197, f32[2048]{0:T(1024)S(1)} %bitcast.46, f32[128]{0:T(128)S(1)} %get-tuple-element.199, f32[2048]{0:T(1024)S(1)} %bitcast.45, ...), kind=kOutput, calls=%fused_computation.2.clone.1 | convolution fusion | flops 104865792 | bytes 337929 | tf_op jit(solution)/shard_map/while/body/eval_jaxpr/while/body/eval_jaxpr/dot_general | solution.py:31
  62.0 1.3 fusion.32
  63.3 58.1 %all-gather.3.cloned.1.call-done = f32[1024,1024]{1,0:T(8,128)} async-done(((f32[32,1024]{1,0:T(8,128)}), f32[1024,1024]{1,0:T(8,128)}) %all-gather.3.cloned.1.call-update) | async-done | bytes 4194320 | tf_op jit(solution)/shard_map/all_gather | solution.py:12
  121.3 2.4 %reduce_sum.18 = f32[32,1024]{1,0:T(8,128)S(1)} reduce(f32[32,32,1024]{2,1,0:T(8,128)} %bitcast.41, f32[]{:T(128)} %constant.57.clone.1), dimensions={0}, to_apply=%region_2.0 | reduce | flops 1015808 | bytes 4325380 | tf_op jit(solution)/shard_map/reduce_sum | solution.py:13
  123.8 2.7 %fusion.27 = f32[32,1,8]{2,1,0:T(1,128)S(1)} fusion(f32[8,32,1024]{2,1,0:T(8,128)S(1)} %copy-done, f32[32,1024,1]{1,0,2:T(8,128)S(1)} %bitcast.42), kind=kOutput, calls=%fused_computation.36 | convolution fusion | flops 3145728 | bytes 1180672 | tf_op jit(solution)/shard_map/jrk,rk->jr/dot_general | solution.py:78
  126.5 0.1 copy.12
  126.6 0.1 copy.13
  126.7 0.4 fusion.29
  127.1 1.5 %fusion.25 = f32[32,1,1024]{2,1,0:T(1,128)S(1)} fusion(f32[8,32,1]{0,2,1:T(1,128)S(1)} %copy.13, f32[8,32,1024]{2,1,0:T(8,128)S(1)} %copy-done), kind=kOutput, calls=%fused_computation.34 | convolution fusion | flops 3145728 | bytes 1180672 | tf_op jit(solution)/shard_map/jr,jrk->rk/dot_general | solution.py:81
  128.6 0.1 multiply_reduce_fusion
  128.8 0.7 broadcast_divide_fusion
  129.5 0.7 subtract_divide_fusion
  (15 shorter events, 0.1 us)
Async XLA Ops:
  7.2 116.6 %copy-start = (f32[8,32,1024]{2,1,0:T(8,128)S(1)}, f32[8,32,1024]{2,1,0:T(8,128)}, u32[]{:S(2)}) copy-start(f32[8,32,1024]{2,1,0:T(8,128)} %param.13) | copy-start | bytes 3145732
  7.2 114.1 %all-gather.3.cloned.1.call-start = ((), (), s32[]{:S(2)}) async-start(), calls=%async_computation | async-start | bytes 4325376 | tf_op jit(solution)/shard_map/all_gather | solution.py:12
  54.7 7.3 %copy-start.1 = (f32[1024,128]{1,0:T(8,128)S(1)}, f32[1024,128]{1,0:T(8,128)}, u32[]{:S(2)}) copy-start(f32[1024,128]{1,0:T(8,128)} %param.12) | copy-start | bytes 1572868
  62.0 64.7 %copy-start.2 = (f32[8,32,128]{2,1,0:T(8,128)S(1)}, f32[8,32,128]{2,1,0:T(8,128)}, u32[]{:S(2)}) copy-start(f32[8,32,128]{2,1,0:T(8,128)} %param.11) | copy-start | bytes 393220
  126.6 3.6 %copy-start.3 = (f32[32,1,8]{0,2,1:T(8,128)}, f32[32,1,8]{0,2,1:T(8,128)S(1)}, u32[]{:S(2)}) copy-start(f32[32,1,8]{0,2,1:T(8,128)S(1)} %copy.12) | copy-start | bytes 3076
  128.7 1.4 %copy-start.4 = (f32[32]{0:T(128)}, f32[32]{0:T(128)S(1)}, u32[]{:S(2)}) copy-start(f32[32]{0:T(128)S(1)} %add_sqrt_fusion) | copy-start | bytes 388
Sparse Core Ops, SparseCore 0:
  63.4 57.9 all-gather.2
